TPU v7x, 256 devices: a whole 4x4x8 slice. The times are simulated.
256 devices in a mesh: gx: 32 (over z, y_lo, core), gy: 8 (over y_hi, x).
Axes of the slice: x: 4, y: 4 (y_hi: 2, y_lo: 2; y = y_hi * 2 + y_lo), z: 8, core: 2. Of those that a mesh axis runs over, the one named last changes fastest.
Arguments:
- right_side: float32 [32, 8, 512, 256], P('gx', 'gy'), may hold values from -8 to 8, as said below
- coords: float32 [32, 8, 2, 512], P('gx', 'gy'), may hold values from 0 to 1
- noise: float32 [32, 8, 512], P('gx', 'gy'), may hold values from 0.25 to 1
- intersect: int32 [32, 8, 128], P('gx', 'gy'), may hold values from 0 to 4607, as said below
Outputs:
- solution: float32 [32, 8, 512, 256], P('gx', 'gy')
- residual: float32 [32, 8, 512, 256], P('gx', 'gy')
Inputs may be any that keep to these rules, and one draw needn't show every extreme that they name: `right_side`: right-hand sides of order one. `intersect`: each subdomain's list holds 128 distinct indices in increasing order; none names the subdomain itself (block number 4) or a subdomain beyond the first or last one along the second dimension.
All inputs are finite; a program needn't handle non-finite values.
Results may differ from a plain program's by a relative error of at most 0.0003.
Values sent between devices are 32-bit elements; how exact they have to be, the bound alone decides.
A program may use at most 128 MiB of HBM per device.

v0:
```python
import math
import jax
import jax.numpy as jnp
from jax import lax
from jax.sharding import Mesh
from jax.sharding import PartitionSpec as P

ITERS = 3
GX = ("gx_0", "gx_1", "gx_2")
GY = ("gy_0", "gy_1")
GX_GY = ("gx_0", "gx_1", "gx_2", "gy_0", "gy_1")
RANGE_LEN = 0.25
ROOT_THREE = math.sqrt(3.0)
HIGH = lax.Precision.HIGHEST


def shifted(value, axis, by):
    count = lax.axis_size(axis)
    return lax.ppermute(value, axis, [(i, (i + by) % count) for i in range(count)])


def passed_along(block, axis, distance):
    devices = range(lax.axis_size(axis))
    route = [(i - distance, i) for i in devices if i - distance in devices]
    return lax.ppermute(block, axis, route)


def over_axes(value, axes):
    for axis in axes:
        value = lax.psum(value, axis)
    return value


def kernel_block(rows_pos, cols_pos):
    delta_x = rows_pos[0][:, None] - cols_pos[0][None, :]
    delta_y = rows_pos[1][:, None] - cols_pos[1][None, :]
    distance = jnp.sqrt(delta_x * delta_x + delta_y * delta_y)
    scaled = ROOT_THREE / RANGE_LEN * distance
    clipped = jnp.minimum(distance, 1.0)
    taper_val = jnp.square(jnp.square(1.0 - clipped)) * (4.0 * clipped + 1.0)
    return (1.0 + scaled) * jnp.exp(-scaled) * taper_val


def window_values(values):
    beside = {}
    for step_by in (1, -1):
        beside[step_by] = shifted(values, GX, step_by)
    column = jnp.stack([beside[1], values, beside[-1]])
    across = {}
    for step_by in (1, -1):
        across[step_by] = passed_along(column, GY, step_by)
    return [across[1], column, across[-1]]


def window_index(values):
    beside = {}
    for step_by in (1, -1):
        beside[step_by] = shifted(values, GX, step_by)
    column = jnp.stack([beside[1], values, beside[-1]])
    across = {}
    for step_by in (1, -1):
        across[step_by] = passed_along(column, GY, step_by)
    return [across[1], column, across[-1]]


def column_sum(first, second):
    return jnp.sum(first * second, axis=0)


def both_sums(residue, precond, image_vec):
    return (
        over_axes(column_sum(residue, precond), GX_GY),
        over_axes(column_sum(image_vec, precond), GX_GY),
    )


def shards(right_side, coords, noise, intersect):
    points = right_side.shape[2]
    rhs_count = right_side.shape[3]
    intersect_len = intersect.shape[2]
    ext_len = points + intersect_len
    own_pos = coords.reshape(2, points)
    own_noise = noise.reshape(points)
    point_info = jnp.concatenate([own_pos, own_noise[None, :]], axis=0)
    info_cols = window_values(point_info)
    positions = [
        [
            jnp.stack(
                [
                    info_cols[col_off][row_off, 0] + float(row_off - 1),
                    info_cols[col_off][row_off, 1] + float(col_off - 1),
                ]
            )
            for col_off in range(3)
        ]
        for row_off in range(3)
    ]
    intersect_ids = intersect.reshape(intersect_len)
    block_id = intersect_ids // points
    row_in = intersect_ids % points
    row_of = block_id // 3
    col_of = block_id % 3
    local_id = row_of * points + row_in
    picked_info = [
        jnp.take(
            jnp.transpose(info_cols[col_off], (1, 0, 2)).reshape(3, 3 * points), local_id, axis=1
        )
        for col_off in range(3)
    ]
    chosen = jnp.where(
        col_of[None, :] == 0,
        picked_info[0],
        jnp.where(col_of[None, :] == 1, picked_info[1], picked_info[2]),
    )
    ov_pos = jnp.stack(
        [chosen[0] + (row_of - 1).astype(jnp.float32), chosen[1] + (col_of - 1).astype(jnp.float32)]
    )
    ext_pos = jnp.concatenate([own_pos, ov_pos], axis=1)
    ext_noise = jnp.concatenate([own_noise, chosen[2]])
    local_matrix = kernel_block(ext_pos, ext_pos) + jnp.diag(ext_noise)
    factor = jnp.linalg.cholesky(local_matrix)
    inv_factor = lax.linalg.triangular_solve(
        factor, jnp.eye(ext_len, dtype=jnp.float32), left_side=True, lower=True
    )
    inverse = jnp.dot(inv_factor.T, inv_factor, precision=HIGH, preferred_element_type=jnp.float32)
    near_ids = window_index(intersect_ids)
    point_iota = jnp.arange(points, dtype=jnp.int32)[:, None]
    row_base = (2 - jnp.arange(3, dtype=jnp.int32))[:, None] * 3
    selectors = []
    for col_off in range(3):
        own_rows = near_ids[col_off] - (row_base + (2 - col_off)) * points
        selectors.append((point_iota == own_rows.reshape(1, 3 * intersect_len)).astype(jnp.float32))

    def borrowed_rows(residue):
        requested = [
            lax.dot_general(
                selectors[col_off],
                residue,
                (((0,), (0,)), ((), ())),
                precision=HIGH,
                preferred_element_type=jnp.float32,
            ).reshape(3, intersect_len, rhs_count)
            for col_off in range(3)
        ]
        combined = jnp.stack([requested[col_off][1] for col_off in range(3)])
        for step_by, row_off in ((-1, 0), (1, 2)):
            outgoing = jnp.stack([requested[col_off][row_off] for col_off in range(3)])
            combined = combined + shifted(outgoing, GX, step_by)
        gathered = combined[1]
        for step_by, col_off in ((-1, 0), (1, 2)):
            gathered = gathered + passed_along(combined[col_off], GY, step_by)
        return gathered

    def precondition(residue):
        gathered = borrowed_rows(residue)
        extended = jnp.concatenate([residue, gathered], axis=0)
        solved = jnp.dot(inverse, extended, precision=HIGH, preferred_element_type=jnp.float32)
        returned = window_values(solved[points:])
        result = solved[:points]
        for col_off in range(3):
            result = result + jnp.dot(
                selectors[col_off],
                returned[col_off].reshape(3 * intersect_len, rhs_count),
                precision=HIGH,
                preferred_element_type=jnp.float32,
            )
        return result

    noise_col = own_noise[:, None]

    def operate(vector):
        columns = window_values(vector)
        accumulated = noise_col * vector
        for row_off in range(3):
            for col_off in range(3):
                accumulated = accumulated + jnp.dot(
                    kernel_block(own_pos, positions[row_off][col_off]),
                    columns[col_off][row_off],
                    precision=HIGH,
                    preferred_element_type=jnp.float32,
                )
        return accumulated

    residual = right_side.reshape(points, rhs_count)
    solution = jnp.zeros_like(residual)
    precond = precondition(residual)
    image_vec = operate(precond)
    gamma_now, curv_sum = both_sums(residual, precond, image_vec)
    step_size = gamma_now / curv_sum
    direction = precond
    image_dir = image_vec
    for iteration in range(ITERS):
        solution = solution + step_size * direction
        residual = residual - step_size * image_dir
        if iteration + 1 < ITERS:
            precond = precondition(residual)
            image_vec = operate(precond)
            gamma_next, curv_sum = both_sums(residual, precond, image_vec)
            beta_val = gamma_next / gamma_now
            step_size = gamma_next / (curv_sum - beta_val * gamma_next / step_size)
            direction = precond + beta_val * direction
            image_dir = image_vec + beta_val * image_dir
            gamma_now = gamma_next
    return (solution.reshape(1, 1, points, rhs_count), residual.reshape(1, 1, points, rhs_count))


def solution(mesh):
    torus = Mesh(mesh.devices.reshape(8, 2, 2, 2, 4), ("gx_0", "gx_1", "gx_2", "gy_0", "gy_1"))
    return jax.shard_map(
        shards,
        mesh=torus,
        in_specs=(P(GX, GY, None, None), P(GX, GY, None, None), P(GX, GY, None), P(GX, GY, None)),
        out_specs=(P(GX, GY, None, None), P(GX, GY, None, None)),
        check_vma=False,
    )
```

profile of v0, /device:TPU:8, one launch (start us, length us, event | category | flops | bytes accessed | tf_op | source)
XLA Modules:
  0.0 719.8 jit_solution(1988938428017498540)
XLA Ops:
  9.0 4.5 collective-permute-start.6
  35.3 11.7 %cholesky.132 = f32[128,128]{1,0:T(8,128)S(1)} custom-call(f32[128,128]{1,0:T(8,128)S(1)} %cholesky.337), custom_call_target="Cholesky" | custom-call | tf_op jit(solution)/shard_map/jit(cholesky)/cholesky | solution.py:121
  47.2 9.8 %custom-call.38 = f32[1,128,128]{1,2,0:T(8,128)S(1)} custom-call(f32[1,128,128]{2,1,0:T(8,128)S(1)} %get-tuple-element.120), custom_call_target="InvertDiagBlocksLowerTriangular" | custom-call | tf_op jit(solution)/shard_map/jit(cholesky)/cholesky | solution.py:121
  59.6 12.1 %cholesky.270 = f32[128,128]{1,0:T(8,128)S(1)} custom-call(f32[128,128]{1,0:T(8,128)S(1)} %cholesky.341), custom_call_target="Cholesky" | custom-call | tf_op jit(solution)/shard_map/jit(cholesky)/cholesky | solution.py:121
  73.2 9.8 %custom-call.39 = f32[1,128,128]{1,2,0:T(8,128)S(1)} custom-call(f32[1,128,128]{2,1,0:T(8,128)S(1)} %get-tuple-element.117), custom_call_target="InvertDiagBlocksLowerTriangular" | custom-call | tf_op jit(solution)/shard_map/jit(cholesky)/cholesky | solution.py:121
  84.7 11.7 %cholesky.291 = f32[128,128]{1,0:T(8,128)S(1)} custom-call(f32[128,128]{1,0:T(8,128)S(1)} %cholesky.346), custom_call_target="Cholesky" | custom-call | tf_op jit(solution)/shard_map/jit(cholesky)/cholesky | solution.py:121
  97.2 9.8 %custom-call.40 = f32[1,128,128]{1,2,0:T(8,128)S(1)} custom-call(f32[1,128,128]{2,1,0:T(8,128)S(1)} %get-tuple-element.114), custom_call_target="InvertDiagBlocksLowerTriangular" | custom-call | tf_op jit(solution)/shard_map/jit(cholesky)/cholesky | solution.py:121
  108.8 11.7 %cholesky.310 = f32[128,128]{1,0:T(8,128)S(1)} custom-call(f32[128,128]{1,0:T(8,128)S(1)} %cholesky.351), custom_call_target="Cholesky" | custom-call | tf_op jit(solution)/shard_map/jit(cholesky)/cholesky | solution.py:121
  121.3 9.8 %custom-call.41 = f32[1,128,128]{1,2,0:T(8,128)S(1)} custom-call(f32[1,128,128]{2,1,0:T(8,128)S(1)} %get-tuple-element.111), custom_call_target="InvertDiagBlocksLowerTriangular" | custom-call | tf_op jit(solution)/shard_map/jit(cholesky)/cholesky | solution.py:121
  132.5 11.7 %cholesky.327 = f32[128,128]{1,0:T(8,128)S(1)} custom-call(f32[128,128]{1,0:T(8,128)S(1)} %convolution_subtract_fusion.6), custom_call_target="Cholesky" | custom-call | tf_op jit(solution)/shard_map/jit(cholesky)/cholesky | solution.py:121
  149.3 17.9 %while.1 = (s32[]{:T(128)}, f32[640,640]{1,0:T(8,128)}, s32[5,2]{0,1:T(2,128)S(1)}, f32[5,128,128]{2,1,0:T(8,128)}, s32[]{:T(128)}) while((s32[]{:T(128)}, f32[640,640]{1,0:T(8,128)}, s32[5,2]{0,1:T(2,128)S(1)}, f32[5,128,128]{2,1,0:T(8,128)}, s32[]{:T(128)}) %tuple.99), condition=%wide.while_cond, body=%wide.while_body.sunk | while | flops 2 | bytes 132705 | solution.py:122
  167.2 50.1 %custom-call.42 = f32[5,128,128]{1,2,0:T(8,128)S(1)} custom-call(f32[5,128,128]{2,1,0:T(8,128)} %get-tuple-element.10), custom_call_target="InvertDiagBlocksLowerTriangular" | custom-call | tf_op jit(solution)/shard_map/triangular_solve | solution.py:122
  228.6 7.2 %collective-permute-start.11 = (f32[128,256]{1,0:T(8,128)S(1)}, f32[128,256]{1,0:T(8,128)S(1)}, u32[]{:S(2)}, u32[]{:S(2)}) collective-permute-start(f32[128,256]{1,0:T(8,128)S(1)} %get-tuple-element.98), channel_id=1, source_target_pairs={{0,1},{1,2},{2,3},{3,4},{4,5},{5,6},{6,7},{8,9},{9,10},{10,11},{11... | collective-permute-start | bytes 393224 | tf_op jit(solution)/shard_map/ppermute | solution.py:25
  235.9 5.0 fusion.241
  245.8 4.0 collective-permute-done.12
  249.8 7.8 %collective-permute-start.14 = (f32[3,128,256]{2,1,0:T(8,128)S(1)}, f32[3,128,256]{2,1,0:T(8,128)S(1)}, u32[]{:S(2)}, u32[]{:S(2)}) collective-permute-start(f32[3,128,256]{2,1,0:T(8,128)S(1)} %pad_maximum_fusion.5), channel_id=1, source_target_pairs={{0,1},{1,2},{2,3},{3,4},{4,5},{5,6},{6,7},{8,9},{9,10},{10,11},{11... | collective-permute-start | bytes 1179656 | tf_op jit(solution)/shard_map/ppermute | solution.py:25
  259.5 5.3 collective-permute-done.14
  265.5 7.4 %collective-permute-done.15 = f32[3,128,256]{2,1,0:T(8,128)S(1)} collective-permute-done((f32[3,128,256]{2,1,0:T(8,128)S(1)}, f32[3,128,256]{2,1,0:T(8,128)S(1)}, u32[]{:S(2)}, u32[]{:S(2)}) %collective-permute-start.15) | collective-permute-done | bytes 393248 | tf_op jit(solution)/shard_map/ppermute | solution.py:25
  275.4 14.8 %collective-permute-done.16 = f32[512,256]{1,0:T(8,128)S(1)} collective-permute-done((f32[512,256]{1,0:T(8,128)S(1)}, f32[512,256]{1,0:T(8,128)S(1)}, u32[]{:S(2)}, u32[]{:S(2)}) %collective-permute-start.16) | collective-permute-done | bytes 524320 | tf_op jit(solution)/shard_map/ppermute | solution.py:19
  290.4 5.2 collective-permute-start.18
  302.8 22.2 %collective-permute-done.18 = f32[3,512,256]{2,1,0:T(8,128)S(1)} collective-permute-done((f32[3,512,256]{2,1,0:T(8,128)S(1)}, f32[3,512,256]{2,1,0:T(8,128)S(1)}, u32[]{:S(2)}, u32[]{:S(2)}) %collective-permute-start.18) | collective-permute-done | bytes 1572896 | tf_op jit(solution)/shard_map/ppermute | solution.py:25
  337.2 18.6 %all-reduce.3 = (f32[256]{0:T(256)S(1)}, f32[256]{0:T(256)S(1)}) all-reduce(f32[256]{0:T(256)S(1)} %get-tuple-element.16, f32[256]{0:T(256)S(1)} %get-tuple-element.15), channel_id=1, replica_groups=mesh['gx_0'=8,'gx_1'=2,'gx_2'=2,'gy_0'=2,'gy_1'=4] {'gx_0'}, use_global_device_ids=true, to_apply=%region_11.13 | all-reduce | flops 512 | bytes 4096 | tf_op jit(solution)/shard_map/psum | solution.py:30
  355.8 4.9 all-reduce.15
  363.2 18.7 %all-reduce.9 = (f32[256]{0:T(256)S(1)}, f32[256]{0:T(256)S(1)}) all-reduce(f32[256]{0:T(256)S(1)} %get-tuple-element.49, f32[256]{0:T(256)S(1)} %get-tuple-element.50), channel_id=1, replica_groups=mesh['gx_0'=8,'gx_1'=2,'gx_2'=2,'gy_0'=2,'gy_1'=4] {'gy_0'}, use_global_device_ids=true, to_apply=%region_14.16 | all-reduce | flops 512 | bytes 4096 | tf_op jit(solution)/shard_map/psum | solution.py:30
  381.9 10.0 %all-reduce.6 = (f32[256]{0:T(256)S(1)}, f32[256]{0:T(256)S(1)}) all-reduce(f32[256]{0:T(256)S(1)} %get-tuple-element.43, f32[256]{0:T(256)S(1)} %get-tuple-element.44), channel_id=1, replica_groups=mesh['gx_0'=8,'gx_1'=2,'gx_2'=2,'gy_0'=2,'gy_1'=4] {'gy_1'}, use_global_device_ids=true, to_apply=%region_15.17 | all-reduce | flops 512 | bytes 4096 | tf_op jit(solution)/shard_map/psum | solution.py:30
  395.3 8.9 %collective-permute-done.20 = f32[3,128,256]{2,1,0:T(8,128)S(1)} collective-permute-done((f32[3,128,256]{2,1,0:T(8,128)S(1)}, f32[3,128,256]{2,1,0:T(8,128)S(1)}, u32[]{:S(2)}, u32[]{:S(2)}) %collective-permute-start.20) | collective-permute-done | bytes 393248 | tf_op jit(solution)/shard_map/ppermute | solution.py:19
  406.5 5.0 collective-permute-start.23
  417.2 3.6 collective-permute-done.24
  420.8 4.4 collective-permute-start.26
  427.1 5.1 collective-permute-done.26
  432.8 3.5 collective-permute-done.27
  440.1 14.4 %collective-permute-done.28 = f32[512,256]{1,0:T(8,128)S(1)} collective-permute-done((f32[512,256]{1,0:T(8,128)S(1)}, f32[512,256]{1,0:T(8,128)S(1)}, u32[]{:S(2)}, u32[]{:S(2)}) %collective-permute-start.28) | collective-permute-done | bytes 524320 | tf_op jit(solution)/shard_map/ppermute | solution.py:19
  463.0 21.2 %collective-permute-done.30 = f32[3,512,256]{2,1,0:T(8,128)S(1)} collective-permute-done((f32[3,512,256]{2,1,0:T(8,128)S(1)}, f32[3,512,256]{2,1,0:T(8,128)S(1)}, u32[]{:S(2)}, u32[]{:S(2)}) %collective-permute-start.30) | collective-permute-done | bytes 1572896 | tf_op jit(solution)/shard_map/ppermute | solution.py:25
  497.3 19.1 %all-reduce.2 = (f32[256]{0:T(256)S(1)}, f32[256]{0:T(256)S(1)}) all-reduce(f32[256]{0:T(256)S(1)} %get-tuple-element.14, f32[256]{0:T(256)S(1)} %get-tuple-element.13), channel_id=1, replica_groups=mesh['gx_0'=8,'gx_1'=2,'gx_2'=2,'gy_0'=2,'gy_1'=4] {'gx_0'}, use_global_device_ids=true, to_apply=%region_23.25 | all-reduce | flops 512 | bytes 4096 | tf_op jit(solution)/shard_map/psum | solution.py:30
  516.5 4.9 all-reduce.14
  523.8 16.4 %all-reduce.8 = (f32[256]{0:T(256)S(1)}, f32[256]{0:T(256)S(1)}) all-reduce(f32[256]{0:T(256)S(1)} %get-tuple-element.47, f32[256]{0:T(256)S(1)} %get-tuple-element.48), channel_id=1, replica_groups=mesh['gx_0'=8,'gx_1'=2,'gx_2'=2,'gy_0'=2,'gy_1'=4] {'gy_0'}, use_global_device_ids=true, to_apply=%region_26.28 | all-reduce | flops 512 | bytes 4096 | tf_op jit(solution)/shard_map/psum | solution.py:30
  540.3 11.2 %all-reduce.5 = (f32[256]{0:T(256)S(1)}, f32[256]{0:T(256)S(1)}) all-reduce(f32[256]{0:T(256)S(1)} %get-tuple-element.41, f32[256]{0:T(256)S(1)} %get-tuple-element.42), channel_id=1, replica_groups=mesh['gx_0'=8,'gx_1'=2,'gx_2'=2,'gy_0'=2,'gy_1'=4] {'gy_1'}, use_global_device_ids=true, to_apply=%region_27.29 | all-reduce | flops 512 | bytes 4096 | tf_op jit(solution)/shard_map/psum | solution.py:30
  555.9 8.9 %collective-permute-done.32 = f32[3,128,256]{2,1,0:T(8,128)S(1)} collective-permute-done((f32[3,128,256]{2,1,0:T(8,128)S(1)}, f32[3,128,256]{2,1,0:T(8,128)S(1)}, u32[]{:S(2)}, u32[]{:S(2)}) %collective-permute-start.32) | collective-permute-done | bytes 393248 | tf_op jit(solution)/shard_map/ppermute | solution.py:19
  568.6 5.0 collective-permute-start.35
  583.0 4.4 collective-permute-start.38
  589.3 7.5 %collective-permute-done.38 = f32[3,128,256]{2,1,0:T(8,128)S(1)} collective-permute-done((f32[3,128,256]{2,1,0:T(8,128)S(1)}, f32[3,128,256]{2,1,0:T(8,128)S(1)}, u32[]{:S(2)}, u32[]{:S(2)}) %collective-permute-start.38) | collective-permute-done | bytes 393248 | tf_op jit(solution)/shard_map/ppermute | solution.py:25
  597.4 3.6 collective-permute-done.39
  603.5 12.6 %collective-permute-done.40 = f32[512,256]{1,0:T(8,128)S(1)} collective-permute-done((f32[512,256]{1,0:T(8,128)S(1)}, f32[512,256]{1,0:T(8,128)S(1)}, u32[]{:S(2)}, u32[]{:S(2)}) %collective-permute-start.40) | collective-permute-done | bytes 524320 | tf_op jit(solution)/shard_map/ppermute | solution.py:19
  625.6 23.0 %collective-permute-done.42 = f32[3,512,256]{2,1,0:T(8,128)S(1)} collective-permute-done((f32[3,512,256]{2,1,0:T(8,128)S(1)}, f32[3,512,256]{2,1,0:T(8,128)S(1)}, u32[]{:S(2)}, u32[]{:S(2)}) %collective-permute-start.42) | collective-permute-done | bytes 1572896 | tf_op jit(solution)/shard_map/ppermute | solution.py:25
  663.8 17.0 %all-reduce.1 = (f32[256]{0:T(256)S(1)}, f32[256]{0:T(256)S(1)}) all-reduce(f32[256]{0:T(256)S(1)} %get-tuple-element.12, f32[256]{0:T(256)S(1)} %get-tuple-element.11), channel_id=1, replica_groups=mesh['gx_0'=8,'gx_1'=2,'gx_2'=2,'gy_0'=2,'gy_1'=4] {'gx_0'}, use_global_device_ids=true, to_apply=%region_35.37 | all-reduce | flops 512 | bytes 4096 | tf_op jit(solution)/shard_map/psum | solution.py:30
  680.7 4.9 all-reduce.13
  688.1 19.2 %all-reduce.7 = (f32[256]{0:T(256)S(1)}, f32[256]{0:T(256)S(1)}) all-reduce(f32[256]{0:T(256)S(1)} %get-tuple-element.45, f32[256]{0:T(256)S(1)} %get-tuple-element.46), channel_id=1, replica_groups=mesh['gx_0'=8,'gx_1'=2,'gx_2'=2,'gy_0'=2,'gy_1'=4] {'gy_0'}, use_global_device_ids=true, to_apply=%region_38.40 | all-reduce | flops 512 | bytes 4096 | tf_op jit(solution)/shard_map/psum | solution.py:30
  707.3 10.0 %all-reduce.4 = (f32[256]{0:T(256)S(1)}, f32[256]{0:T(256)S(1)}) all-reduce(f32[256]{0:T(256)S(1)} %get-tuple-element.39, f32[256]{0:T(256)S(1)} %get-tuple-element.40), channel_id=1, replica_groups=mesh['gx_0'=8,'gx_1'=2,'gx_2'=2,'gy_0'=2,'gy_1'=4] {'gy_1'}, use_global_device_ids=true, to_apply=%region_39.41 | all-reduce | flops 512 | bytes 4096 | tf_op jit(solution)/shard_map/psum | solution.py:30
  (301 shorter events, 196.5 us)
Async XLA Ops:
  0.7 6.9 collective-permute-start.4
  0.7 6.8 collective-permute-start.5
  3.2 16.9 %collective-permute-start = (f32[3,512]{1,0:T(4,128)S(1)}, f32[3,512]{1,0:T(4,128)S(1)}, u32[]{:S(2)}, u32[]{:S(2)}) collective-permute-start(f32[3,512]{1,0:T(4,128)S(1)} %get-tuple-element.147), channel_id=1, source_target_pairs={{0,8},{8,16},{16,24},{24,32},{32,40},{40,48},{48,56},{56,64},{64,7... | collective-permute-start | bytes 18440 | tf_op jit(solution)/shard_map/ppermute | solution.py:19
  3.4 16.6 %collective-permute-start.1 = (f32[3,512]{1,0:T(4,128)S(1)}, f32[3,512]{1,0:T(4,128)S(1)}, u32[]{:S(2)}, u32[]{:S(2)}) collective-permute-start(f32[3,512]{1,0:T(4,128)S(1)} %get-tuple-element.147), channel_id=1, source_target_pairs={{0,248},{8,0},{16,8},{24,16},{32,24},{40,32},{48,40},{56,48},{64,5... | collective-permute-start | bytes 18440 | tf_op jit(solution)/shard_map/ppermute | solution.py:19
  7.7 6.7 collective-permute-start.7
  9.0 6.3 collective-permute-start.6
  17.1 209.0 %collective-permute-start.8 = (f32[3,128,256]{2,1,0:T(8,128)}, f32[3,128,256]{2,1,0:T(8,128)}, u32[]{:S(2)}, u32[]{:S(2)}) collective-permute-start(f32[3,128,256]{2,1,0:T(8,128)} %pad_maximum_fusion.3), channel_id=1, source_target_pairs={{0,248},{8,0},{16,8},{24,16},{32,24},{40,32},{48,40},{56,48},{64,5... | collective-permute-start | bytes 1179656 | tf_op jit(solution)/shard_map/ppermute | solution.py:19
  20.1 6.6 collective-permute-start.2
  23.5 5.7 collective-permute-start.3
  25.6 200.5 %collective-permute-start.9 = (f32[3,128,256]{2,1,0:T(8,128)}, f32[3,128,256]{2,1,0:T(8,128)}, u32[]{:S(2)}, u32[]{:S(2)}) collective-permute-start(f32[3,128,256]{2,1,0:T(8,128)} %pad_maximum_fusion.4), channel_id=1, source_target_pairs={{0,8},{8,16},{16,24},{24,32},{32,40},{40,48},{48,56},{56,64},{64,7... | collective-permute-start | bytes 1179656 | tf_op jit(solution)/shard_map/ppermute | solution.py:19
  227.3 13.6 %collective-permute-start.10 = (f32[128,256]{1,0:T(8,128)S(1)}, f32[128,256]{1,0:T(8,128)S(1)}, u32[]{:S(2)}, u32[]{:S(2)}) collective-permute-start(f32[128,256]{1,0:T(8,128)S(1)} %get-tuple-element.97), channel_id=1, source_target_pairs={{1,0},{2,1},{3,2},{4,3},{5,4},{6,5},{7,6},{9,8},{10,9},{11,10},{12... | collective-permute-start | bytes 393224 | tf_op jit(solution)/shard_map/ppermute | solution.py:25
  228.6 12.3 %collective-permute-start.11 = (f32[128,256]{1,0:T(8,128)S(1)}, f32[128,256]{1,0:T(8,128)S(1)}, u32[]{:S(2)}, u32[]{:S(2)}) collective-permute-start(f32[128,256]{1,0:T(8,128)S(1)} %get-tuple-element.98), channel_id=1, source_target_pairs={{0,1},{1,2},{2,3},{3,4},{4,5},{5,6},{6,7},{8,9},{9,10},{10,11},{11... | collective-permute-start | bytes 393224 | tf_op jit(solution)/shard_map/ppermute | solution.py:25
  242.8 7.0 collective-permute-start.12
  242.8 6.9 collective-permute-start.13
  249.8 15.0 %collective-permute-start.14 = (f32[3,128,256]{2,1,0:T(8,128)S(1)}, f32[3,128,256]{2,1,0:T(8,128)S(1)}, u32[]{:S(2)}, u32[]{:S(2)}) collective-permute-start(f32[3,128,256]{2,1,0:T(8,128)S(1)} %pad_maximum_fusion.5), channel_id=1, source_target_pairs={{0,1},{1,2},{2,3},{3,4},{4,5},{5,6},{6,7},{8,9},{9,10},{10,11},{11... | collective-permute-start | bytes 1179656 | tf_op jit(solution)/shard_map/ppermute | solution.py:25
  257.6 15.3 %collective-permute-start.15 = (f32[3,128,256]{2,1,0:T(8,128)S(1)}, f32[3,128,256]{2,1,0:T(8,128)S(1)}, u32[]{:S(2)}, u32[]{:S(2)}) collective-permute-start(f32[3,128,256]{2,1,0:T(8,128)S(1)} %pad_maximum_fusion.5), channel_id=1, source_target_pairs={{1,0},{2,1},{3,2},{4,3},{5,4},{6,5},{7,6},{9,8},{10,9},{11,10},{12... | collective-permute-start | bytes 1179656 | tf_op jit(solution)/shard_map/ppermute | solution.py:25
  273.5 61.6 %copy-start.1 = (f32[512,256]{1,0:T(8,128)}, f32[512,256]{1,0:T(8,128)S(1)}, u32[]{:S(2)}) copy-start(f32[512,256]{1,0:T(8,128)S(1)} %convolution_add_fusion.5) | copy-start | bytes 1572868
  273.6 16.7 %collective-permute-start.16 = (f32[512,256]{1,0:T(8,128)S(1)}, f32[512,256]{1,0:T(8,128)S(1)}, u32[]{:S(2)}, u32[]{:S(2)}) collective-permute-start(f32[512,256]{1,0:T(8,128)S(1)} %convolution_add_fusion.5), channel_id=1, source_target_pairs={{0,8},{8,16},{16,24},{24,32},{32,40},{40,48},{48,56},{56,64},{64,7... | collective-permute-start | bytes 1572872 | tf_op jit(solution)/shard_map/ppermute | solution.py:19
  273.7 16.6 %collective-permute-start.17 = (f32[512,256]{1,0:T(8,128)S(1)}, f32[512,256]{1,0:T(8,128)S(1)}, u32[]{:S(2)}, u32[]{:S(2)}) collective-permute-start(f32[512,256]{1,0:T(8,128)S(1)} %convolution_add_fusion.5), channel_id=1, source_target_pairs={{0,248},{8,0},{16,8},{24,16},{32,24},{40,32},{48,40},{56,48},{64,5... | collective-permute-start | bytes 1572872 | tf_op jit(solution)/shard_map/ppermute | solution.py:19
  290.4 34.6 %collective-permute-start.18 = (f32[3,512,256]{2,1,0:T(8,128)S(1)}, f32[3,512,256]{2,1,0:T(8,128)S(1)}, u32[]{:S(2)}, u32[]{:S(2)}) collective-permute-start(f32[3,512,256]{2,1,0:T(8,128)S(1)} %pad_maximum_fusion), channel_id=1, source_target_pairs={{0,1},{1,2},{2,3},{3,4},{4,5},{5,6},{6,7},{8,9},{9,10},{10,11},{11... | collective-permute-start | bytes 4718600 | tf_op jit(solution)/shard_map/ppermute | solution.py:25
  295.7 35.4 %collective-permute-start.19 = (f32[3,512,256]{2,1,0:T(8,128)S(1)}, f32[3,512,256]{2,1,0:T(8,128)S(1)}, u32[]{:S(2)}, u32[]{:S(2)}) collective-permute-start(f32[3,512,256]{2,1,0:T(8,128)S(1)} %pad_maximum_fusion), channel_id=1, source_target_pairs={{1,0},{2,1},{3,2},{4,3},{5,4},{6,5},{7,6},{9,8},{10,9},{11,10},{12... | collective-permute-start | bytes 4718600 | tf_op jit(solution)/shard_map/ppermute | solution.py:25
  394.6 9.6 %collective-permute-start.20 = (f32[3,128,256]{2,1,0:T(8,128)S(1)}, f32[3,128,256]{2,1,0:T(8,128)S(1)}, u32[]{:S(2)}, u32[]{:S(2)}) collective-permute-start(f32[3,128,256]{2,1,0:T(8,128)S(1)} %pad_maximum_fusion.6), channel_id=1, source_target_pairs={{0,248},{8,0},{16,8},{24,16},{32,24},{40,32},{48,40},{56,48},{64,5... | collective-permute-start | bytes 1179656 | tf_op jit(solution)/shard_map/ppermute | solution.py:19
  394.7 10.4 %collective-permute-start.21 = (f32[3,128,256]{2,1,0:T(8,128)S(1)}, f32[3,128,256]{2,1,0:T(8,128)S(1)}, u32[]{:S(2)}, u32[]{:S(2)}) collective-permute-start(f32[3,128,256]{2,1,0:T(8,128)S(1)} %pad_maximum_fusion.7), channel_id=1, source_target_pairs={{0,8},{8,16},{16,24},{24,32},{32,40},{40,48},{48,56},{56,64},{64,7... | collective-permute-start | bytes 1179656 | tf_op jit(solution)/shard_map/ppermute | solution.py:19
  405.2 6.9 collective-permute-start.22
  406.5 7.1 collective-permute-start.23
  415.3 5.4 collective-permute-start.24
  415.4 5.3 collective-permute-start.25
  420.8 11.4 %collective-permute-start.26 = (f32[3,128,256]{2,1,0:T(8,128)S(1)}, f32[3,128,256]{2,1,0:T(8,128)S(1)}, u32[]{:S(2)}, u32[]{:S(2)}) collective-permute-start(f32[3,128,256]{2,1,0:T(8,128)S(1)} %pad_maximum_fusion.8), channel_id=1, source_target_pairs={{0,1},{1,2},{2,3},{3,4},{4,5},{5,6},{6,7},{8,9},{9,10},{10,11},{11... | collective-permute-start | bytes 1179656 | tf_op jit(solution)/shard_map/ppermute | solution.py:25
  425.2 11.1 %collective-permute-start.27 = (f32[3,128,256]{2,1,0:T(8,128)S(1)}, f32[3,128,256]{2,1,0:T(8,128)S(1)}, u32[]{:S(2)}, u32[]{:S(2)}) collective-permute-start(f32[3,128,256]{2,1,0:T(8,128)S(1)} %pad_maximum_fusion.8), channel_id=1, source_target_pairs={{1,0},{2,1},{3,2},{4,3},{5,4},{6,5},{7,6},{9,8},{10,9},{11,10},{12... | collective-permute-start | bytes 1179656 | tf_op jit(solution)/shard_map/ppermute | solution.py:25
  437.0 57.5 %copy-start.3 = (f32[512,256]{1,0:T(8,128)}, f32[512,256]{1,0:T(8,128)S(1)}, u32[]{:S(2)}) copy-start(f32[512,256]{1,0:T(8,128)S(1)} %convolution_add_fusion.4) | copy-start | bytes 1572868
  437.0 17.5 %collective-permute-start.28 = (f32[512,256]{1,0:T(8,128)S(1)}, f32[512,256]{1,0:T(8,128)S(1)}, u32[]{:S(2)}, u32[]{:S(2)}) collective-permute-start(f32[512,256]{1,0:T(8,128)S(1)} %convolution_add_fusion.4), channel_id=1, source_target_pairs={{0,8},{8,16},{16,24},{24,32},{32,40},{40,48},{48,56},{56,64},{64,7... | collective-permute-start | bytes 1572872 | tf_op jit(solution)/shard_map/ppermute | solution.py:19
  437.1 17.4 %collective-permute-start.29 = (f32[512,256]{1,0:T(8,128)S(1)}, f32[512,256]{1,0:T(8,128)S(1)}, u32[]{:S(2)}, u32[]{:S(2)}) collective-permute-start(f32[512,256]{1,0:T(8,128)S(1)} %convolution_add_fusion.4), channel_id=1, source_target_pairs={{0,248},{8,0},{16,8},{24,16},{32,24},{40,32},{48,40},{56,48},{64,5... | collective-permute-start | bytes 1572872 | tf_op jit(solution)/shard_map/ppermute | solution.py:19
  454.6 29.7 %collective-permute-start.30 = (f32[3,512,256]{2,1,0:T(8,128)S(1)}, f32[3,512,256]{2,1,0:T(8,128)S(1)}, u32[]{:S(2)}, u32[]{:S(2)}) collective-permute-start(f32[3,512,256]{2,1,0:T(8,128)S(1)} %pad_maximum_fusion.1), channel_id=1, source_target_pairs={{0,1},{1,2},{2,3},{3,4},{4,5},{5,6},{6,7},{8,9},{9,10},{10,11},{11... | collective-permute-start | bytes 4718600 | tf_op jit(solution)/shard_map/ppermute | solution.py:25
  456.0 34.5 %collective-permute-start.31 = (f32[3,512,256]{2,1,0:T(8,128)S(1)}, f32[3,512,256]{2,1,0:T(8,128)S(1)}, u32[]{:S(2)}, u32[]{:S(2)}) collective-permute-start(f32[3,512,256]{2,1,0:T(8,128)S(1)} %pad_maximum_fusion.1), channel_id=1, source_target_pairs={{1,0},{2,1},{3,2},{4,3},{5,4},{6,5},{7,6},{9,8},{10,9},{11,10},{12... | collective-permute-start | bytes 4718600 | tf_op jit(solution)/shard_map/ppermute | solution.py:25
  555.2 9.6 %collective-permute-start.32 = (f32[3,128,256]{2,1,0:T(8,128)S(1)}, f32[3,128,256]{2,1,0:T(8,128)S(1)}, u32[]{:S(2)}, u32[]{:S(2)}) collective-permute-start(f32[3,128,256]{2,1,0:T(8,128)S(1)} %pad_maximum_fusion.9), channel_id=1, source_target_pairs={{0,248},{8,0},{16,8},{24,16},{32,24},{40,32},{48,40},{56,48},{64,5... | collective-permute-start | bytes 1179656 | tf_op jit(solution)/shard_map/ppermute | solution.py:19
  555.3 11.9 %collective-permute-start.33 = (f32[3,128,256]{2,1,0:T(8,128)S(1)}, f32[3,128,256]{2,1,0:T(8,128)S(1)}, u32[]{:S(2)}, u32[]{:S(2)}) collective-permute-start(f32[3,128,256]{2,1,0:T(8,128)S(1)} %pad_maximum_fusion.10), channel_id=1, source_target_pairs={{0,8},{8,16},{16,24},{24,32},{32,40},{40,48},{48,56},{56,64},{64,7... | collective-permute-start | bytes 1179656 | tf_op jit(solution)/shard_map/ppermute | solution.py:19
  567.3 6.9 collective-permute-start.34
  568.6 7.1 collective-permute-start.35
  577.4 4.5 collective-permute-start.36
  577.5 5.4 collective-permute-start.37
  583.0 13.8 %collective-permute-start.38 = (f32[3,128,256]{2,1,0:T(8,128)S(1)}, f32[3,128,256]{2,1,0:T(8,128)S(1)}, u32[]{:S(2)}, u32[]{:S(2)}) collective-permute-start(f32[3,128,256]{2,1,0:T(8,128)S(1)} %pad_maximum_fusion.11), channel_id=1, source_target_pairs={{0,1},{1,2},{2,3},{3,4},{4,5},{5,6},{6,7},{8,9},{9,10},{10,11},{11... | collective-permute-start | bytes 1179656 | tf_op jit(solution)/shard_map/ppermute | solution.py:25
  587.4 13.6 %collective-permute-start.39 = (f32[3,128,256]{2,1,0:T(8,128)S(1)}, f32[3,128,256]{2,1,0:T(8,128)S(1)}, u32[]{:S(2)}, u32[]{:S(2)}) collective-permute-start(f32[3,128,256]{2,1,0:T(8,128)S(1)} %pad_maximum_fusion.11), channel_id=1, source_target_pairs={{1,0},{2,1},{3,2},{4,3},{5,4},{6,5},{7,6},{9,8},{10,9},{11,10},{12... | collective-permute-start | bytes 1179656 | tf_op jit(solution)/shard_map/ppermute | solution.py:25
  601.7 14.4 %collective-permute-start.40 = (f32[512,256]{1,0:T(8,128)S(1)}, f32[512,256]{1,0:T(8,128)S(1)}, u32[]{:S(2)}, u32[]{:S(2)}) collective-permute-start(f32[512,256]{1,0:T(8,128)S(1)} %convolution_add_fusion.3), channel_id=1, source_target_pairs={{0,8},{8,16},{16,24},{24,32},{32,40},{40,48},{48,56},{56,64},{64,7... | collective-permute-start | bytes 1572872 | tf_op jit(solution)/shard_map/ppermute | solution.py:19
  601.8 14.4 %collective-permute-start.41 = (f32[512,256]{1,0:T(8,128)S(1)}, f32[512,256]{1,0:T(8,128)S(1)}, u32[]{:S(2)}, u32[]{:S(2)}) collective-permute-start(f32[512,256]{1,0:T(8,128)S(1)} %convolution_add_fusion.3), channel_id=1, source_target_pairs={{0,248},{8,0},{16,8},{24,16},{32,24},{40,32},{48,40},{56,48},{64,5... | collective-permute-start | bytes 1572872 | tf_op jit(solution)/shard_map/ppermute | solution.py:19
  616.2 32.4 %collective-permute-start.42 = (f32[3,512,256]{2,1,0:T(8,128)S(1)}, f32[3,512,256]{2,1,0:T(8,128)S(1)}, u32[]{:S(2)}, u32[]{:S(2)}) collective-permute-start(f32[3,512,256]{2,1,0:T(8,128)S(1)} %pad_maximum_fusion.2), channel_id=1, source_target_pairs={{0,1},{1,2},{2,3},{3,4},{4,5},{5,6},{6,7},{8,9},{9,10},{10,11},{11... | collective-permute-start | bytes 4718600 | tf_op jit(solution)/shard_map/ppermute | solution.py:25
  618.6 38.4 %collective-permute-start.43 = (f32[3,512,256]{2,1,0:T(8,128)S(1)}, f32[3,512,256]{2,1,0:T(8,128)S(1)}, u32[]{:S(2)}, u32[]{:S(2)}) collective-permute-start(f32[3,512,256]{2,1,0:T(8,128)S(1)} %pad_maximum_fusion.2), channel_id=1, source_target_pairs={{1,0},{2,1},{3,2},{4,3},{5,4},{6,5},{7,6},{9,8},{10,9},{11,10},{12... | collective-permute-start | bytes 4718600 | tf_op jit(solution)/shard_map/ppermute | solution.py:25
  660.8 56.5 %copy-start.2 = (f32[512,256]{1,0:T(8,128)S(1)}, f32[512,256]{1,0:T(8,128)}, u32[]{:S(2)}) copy-start(f32[512,256]{1,0:T(8,128)} %copy-done.1) | copy-start | bytes 1572868
  660.8 56.4 %copy-start.4 = (f32[512,256]{1,0:T(8,128)S(1)}, f32[512,256]{1,0:T(8,128)}, u32[]{:S(2)}) copy-start(f32[512,256]{1,0:T(8,128)} %copy-done.3) | copy-start | bytes 1572868
  (25 other events, 361.8 us)
where the time goes:
time: 727 us; the launch traced here: 720 us
  waiting for transfers between devices  183 us (25%)
  other arithmetic  167 us (23%)
  blocking collectives  162 us (22%)
  matrix products  92.3 us (13%)
  starting transfers between devices  86.8 us (12%)
  local copies, waits for them, and re-layouts  23.7 us (3%)
    psum x15, blocking collectives, over_axes(): value = lax.psum(value, axis)  162 us
    ppermute x22, waiting for transfers between devices, passed_along(): return lax.ppermute(block, axis, route)  108 us
    another operation x19, other arithmetic, shards(): factor = jnp.linalg.cholesky(local_matrix)  102 us
    ppermute x22, waiting for transfers between devices, shifted(): lax.ppermute(value, axis, [(i, (i + by) % count) for i in range(count)])  74.3 us
    ppermute x22, starting transfers between devices, passed_along(): return lax.ppermute(block, axis, route)  65.3 us
    dot_general x27, matrix products, operate(): jnp.dot(kernel_block(own_pos, positions[row_off][col_off]), columns[col_o...  52.9 us
    another operation x3, other arithmetic, shards(): lax.linalg.triangular_solve(factor, jnp.eye(ext_len, dtype=jnp.float32),...  51.4 us
    ppermute x22, starting transfers between devices, shifted(): lax.ppermute(value, axis, [(i, (i + by) % count) for i in range(count)])  21.5 us
  transfers between devices with their start and end apart: 44, of which 28 were waited for; matrix products, arithmetic and copies ran while one was open for 34% of the time, Pallas kernels for 0%

commit v1 on v0

--- a/solution.py
+++ b/solution.py
@@ -27,7 +27,7 @@
 
 def over_axes(value, axes):
     for axis in axes:
-        value = lax.psum(value, axis)
+        value = jnp.sum(lax.all_gather(value, axis), axis=0)
     return value
 
 

time: 727 us -> 815 us (1.12)
  blocking collectives: 162 us -> 246 us
    all_gather x0 -> x30, blocking collectives: none -> 246 us  [over_axes(): value = jnp.sum(lax.all_gather(value, axis), axis=0)]
    psum x15 -> x0, blocking collectives: 162 us -> none  [over_axes(): value = lax.psum(value, axis)]
  transfers between devices with their start and end apart: 44 -> 44, of which waited for: 28 -> 27; matrix products, arithmetic and copies ran while one was open for 34% -> 30% of each run, Pallas kernels for 0% -> 0%
where the time goes in v1:
time: 815 us; the launch traced here: 806 us
  blocking collectives  246 us (30%)
  waiting for transfers between devices  187 us (23%)
  other arithmetic  167 us (20%)
  matrix products  92.3 us (11%)
  starting transfers between devices  83.8 us (10%)
  local copies, waits for them, and re-layouts  23.5 us (3%)
    all_gather x30, blocking collectives, over_axes(): value = jnp.sum(lax.all_gather(value, axis), axis=0)  246 us
    ppermute x22, waiting for transfers between devices, passed_along(): return lax.ppermute(block, axis, route)  105 us
    another operation x19, other arithmetic, shards(): factor = jnp.linalg.cholesky(local_matrix)  102 us
    ppermute x22, waiting for transfers between devices, shifted(): lax.ppermute(value, axis, [(i, (i + by) % count) for i in range(count)])  82.2 us
    ppermute x22, starting transfers between devices, passed_along(): return lax.ppermute(block, axis, route)  61.7 us
    dot_general x27, matrix products, operate(): jnp.dot(kernel_block(own_pos, positions[row_off][col_off]), columns[col_o...  52.9 us
    another operation x3, other arithmetic, shards(): lax.linalg.triangular_solve(factor, jnp.eye(ext_len, dtype=jnp.float32),...  51.4 us
    ppermute x22, starting transfers between devices, shifted(): lax.ppermute(value, axis, [(i, (i + by) % count) for i in range(count)])  22.1 us
  transfers between devices with their start and end apart: 44, of which 27 were waited for; matrix products, arithmetic and copies ran while one was open for 30% of the time, Pallas kernels for 0%

profile of v1, /device:TPU:8, one launch (start us, length us, event | category | flops | bytes accessed | tf_op | source)
XLA Modules:
  0.0 805.9 jit_solution(7705376196644096273)
XLA Ops:
  35.3 11.7 %cholesky.132 = f32[128,128]{1,0:T(8,128)S(1)} custom-call(f32[128,128]{1,0:T(8,128)S(1)} %cholesky.337), custom_call_target="Cholesky" | custom-call | tf_op jit(solution)/shard_map/jit(cholesky)/cholesky | solution.py:121
  47.1 9.8 %custom-call.38 = f32[1,128,128]{1,2,0:T(8,128)S(1)} custom-call(f32[1,128,128]{2,1,0:T(8,128)S(1)} %get-tuple-element.90), custom_call_target="InvertDiagBlocksLowerTriangular" | custom-call | tf_op jit(solution)/shard_map/jit(cholesky)/cholesky | solution.py:121
  59.6 12.1 %cholesky.270 = f32[128,128]{1,0:T(8,128)S(1)} custom-call(f32[128,128]{1,0:T(8,128)S(1)} %cholesky.341), custom_call_target="Cholesky" | custom-call | tf_op jit(solution)/shard_map/jit(cholesky)/cholesky | solution.py:121
  73.1 9.8 %custom-call.39 = f32[1,128,128]{1,2,0:T(8,128)S(1)} custom-call(f32[1,128,128]{2,1,0:T(8,128)S(1)} %get-tuple-element.87), custom_call_target="InvertDiagBlocksLowerTriangular" | custom-call | tf_op jit(solution)/shard_map/jit(cholesky)/cholesky | solution.py:121
  84.7 11.7 %cholesky.291 = f32[128,128]{1,0:T(8,128)S(1)} custom-call(f32[128,128]{1,0:T(8,128)S(1)} %cholesky.346), custom_call_target="Cholesky" | custom-call | tf_op jit(solution)/shard_map/jit(cholesky)/cholesky | solution.py:121
  97.1 9.8 %custom-call.40 = f32[1,128,128]{1,2,0:T(8,128)S(1)} custom-call(f32[1,128,128]{2,1,0:T(8,128)S(1)} %get-tuple-element.84), custom_call_target="InvertDiagBlocksLowerTriangular" | custom-call | tf_op jit(solution)/shard_map/jit(cholesky)/cholesky | solution.py:121
  108.8 11.7 %cholesky.310 = f32[128,128]{1,0:T(8,128)S(1)} custom-call(f32[128,128]{1,0:T(8,128)S(1)} %cholesky.351), custom_call_target="Cholesky" | custom-call | tf_op jit(solution)/shard_map/jit(cholesky)/cholesky | solution.py:121
  121.2 9.8 %custom-call.41 = f32[1,128,128]{1,2,0:T(8,128)S(1)} custom-call(f32[1,128,128]{2,1,0:T(8,128)S(1)} %get-tuple-element.81), custom_call_target="InvertDiagBlocksLowerTriangular" | custom-call | tf_op jit(solution)/shard_map/jit(cholesky)/cholesky | solution.py:121
  132.5 11.7 %cholesky.327 = f32[128,128]{1,0:T(8,128)S(1)} custom-call(f32[128,128]{1,0:T(8,128)S(1)} %convolution_subtract_fusion.6), custom_call_target="Cholesky" | custom-call | tf_op jit(solution)/shard_map/jit(cholesky)/cholesky | solution.py:121
  149.2 17.7 %while.1 = (s32[]{:T(128)}, f32[640,640]{1,0:T(8,128)}, s32[5,2]{0,1:T(2,128)S(1)}, f32[5,128,128]{2,1,0:T(8,128)}, s32[]{:T(128)}) while((s32[]{:T(128)}, f32[640,640]{1,0:T(8,128)}, s32[5,2]{0,1:T(2,128)S(1)}, f32[5,128,128]{2,1,0:T(8,128)}, s32[]{:T(128)}) %tuple.99), condition=%wide.while_cond, body=%wide.while_body.sunk | while | flops 2 | bytes 132705 | solution.py:122
  166.9 50.1 %custom-call.42 = f32[5,128,128]{1,2,0:T(8,128)S(1)} custom-call(f32[5,128,128]{2,1,0:T(8,128)} %get-tuple-element.10), custom_call_target="InvertDiagBlocksLowerTriangular" | custom-call | tf_op jit(solution)/shard_map/triangular_solve | solution.py:122
  228.4 7.2 collective-permute-start.11
  235.6 5.0 fusion.241
  249.6 7.8 collective-permute-start.14
  259.3 5.3 collective-permute-done.14
  265.2 7.4 collective-permute-done.15
  275.2 14.8 %collective-permute-done.16 = f32[512,256]{1,0:T(8,128)S(1)} collective-permute-done((f32[512,256]{1,0:T(8,128)S(1)}, f32[512,256]{1,0:T(8,128)S(1)}, u32[]{:S(2)}, u32[]{:S(2)}) %collective-permute-start.16) | collective-permute-done | bytes 524320 | tf_op jit(solution)/shard_map/ppermute | solution.py:19
  290.1 5.2 collective-permute-start.18
  302.5 22.2 %collective-permute-done.18 = f32[3,512,256]{2,1,0:T(8,128)S(1)} collective-permute-done((f32[3,512,256]{2,1,0:T(8,128)S(1)}, f32[3,512,256]{2,1,0:T(8,128)S(1)}, u32[]{:S(2)}, u32[]{:S(2)}) %collective-permute-start.18) | collective-permute-done | bytes 1572896 | tf_op jit(solution)/shard_map/ppermute | solution.py:25
  336.9 17.8 %all-gather.30 = f32[8,1,256]{2,1,0:T(1,128)S(1)} all-gather(f32[1,1,256]{2,1,0:T(1,128)S(1)} %bitcast.548), channel_id=2, replica_groups=mesh['gx_0'=8,'gx_1'=2,'gx_2'=2,'gy_0'=2,'gy_1'=4] {'gx_0'}, dimensions={0}, use_global_device_ids=true | all-gather | bytes 9216 | tf_op jit(solution)/shard_map/all_gather | solution.py:30
  360.8 18.0 %all-gather.33 = f32[2,1,256]{2,1,0:T(1,128)S(1)} all-gather(f32[1,1,256]{2,1,0:T(1,128)S(1)} %bitcast.414), channel_id=5, replica_groups=mesh['gx_0'=8,'gx_1'=2,'gx_2'=2,'gy_0'=2,'gy_1'=4] {'gy_0'}, dimensions={0}, use_global_device_ids=true | all-gather | bytes 3072 | tf_op jit(solution)/shard_map/all_gather | solution.py:30
  378.8 9.3 %all-gather.34 = f32[4,1,256]{2,1,0:T(1,128)S(1)} all-gather(f32[1,1,256]{2,1,0:T(1,128)S(1)} %bitcast.415), channel_id=6, replica_groups=mesh['gx_0'=8,'gx_1'=2,'gx_2'=2,'gy_0'=2,'gy_1'=4] {'gy_1'}, dimensions={0}, use_global_device_ids=true | all-gather | bytes 5120 | tf_op jit(solution)/shard_map/all_gather | solution.py:30
  388.2 14.4 %all-gather.35 = f32[8,1,256]{2,1,0:T(1,128)S(1)} all-gather(f32[1,1,256]{2,1,0:T(1,128)S(1)} %bitcast.545), channel_id=7, replica_groups=mesh['gx_0'=8,'gx_1'=2,'gx_2'=2,'gy_0'=2,'gy_1'=4] {'gx_0'}, dimensions={0}, use_global_device_ids=true | all-gather | bytes 9216 | tf_op jit(solution)/shard_map/all_gather | solution.py:30
  408.6 5.7 all-gather.38
  414.4 7.0 all-gather.39
  424.8 8.9 %collective-permute-done.20 = f32[3,128,256]{2,1,0:T(8,128)S(1)} collective-permute-done((f32[3,128,256]{2,1,0:T(8,128)S(1)}, f32[3,128,256]{2,1,0:T(8,128)S(1)}, u32[]{:S(2)}, u32[]{:S(2)}) %collective-permute-start.20) | collective-permute-done | bytes 393248 | tf_op jit(solution)/shard_map/ppermute | solution.py:19
  446.9 5.0 collective-permute-done.24
  456.8 5.1 collective-permute-done.26
  469.8 15.6 %collective-permute-done.28 = f32[512,256]{1,0:T(8,128)S(1)} collective-permute-done((f32[512,256]{1,0:T(8,128)S(1)}, f32[512,256]{1,0:T(8,128)S(1)}, u32[]{:S(2)}, u32[]{:S(2)}) %collective-permute-start.28) | collective-permute-done | bytes 524320 | tf_op jit(solution)/shard_map/ppermute | solution.py:19
  494.0 21.2 %collective-permute-done.30 = f32[3,512,256]{2,1,0:T(8,128)S(1)} collective-permute-done((f32[3,512,256]{2,1,0:T(8,128)S(1)}, f32[3,512,256]{2,1,0:T(8,128)S(1)}, u32[]{:S(2)}, u32[]{:S(2)}) %collective-permute-start.30) | collective-permute-done | bytes 1572896 | tf_op jit(solution)/shard_map/ppermute | solution.py:25
  529.7 20.4 %all-gather.40 = f32[8,1,256]{2,1,0:T(1,128)S(1)} all-gather(f32[1,1,256]{2,1,0:T(1,128)S(1)} %bitcast.549), channel_id=12, replica_groups=mesh['gx_0'=8,'gx_1'=2,'gx_2'=2,'gy_0'=2,'gy_1'=4] {'gx_0'}, dimensions={0}, use_global_device_ids=true | all-gather | bytes 9216 | tf_op jit(solution)/shard_map/all_gather | solution.py:30
  556.3 12.0 %all-gather.43 = f32[2,1,256]{2,1,0:T(1,128)S(1)} all-gather(f32[1,1,256]{2,1,0:T(1,128)S(1)} %bitcast.422), channel_id=15, replica_groups=mesh['gx_0'=8,'gx_1'=2,'gx_2'=2,'gy_0'=2,'gy_1'=4] {'gy_0'}, dimensions={0}, use_global_device_ids=true | all-gather | bytes 3072 | tf_op jit(solution)/shard_map/all_gather | solution.py:30
  568.3 9.3 %all-gather.44 = f32[4,1,256]{2,1,0:T(1,128)S(1)} all-gather(f32[1,1,256]{2,1,0:T(1,128)S(1)} %bitcast.423), channel_id=16, replica_groups=mesh['gx_0'=8,'gx_1'=2,'gx_2'=2,'gy_0'=2,'gy_1'=4] {'gy_1'}, dimensions={0}, use_global_device_ids=true | all-gather | bytes 5120 | tf_op jit(solution)/shard_map/all_gather | solution.py:30
  577.6 15.3 %all-gather.45 = f32[8,1,256]{2,1,0:T(1,128)S(1)} all-gather(f32[1,1,256]{2,1,0:T(1,128)S(1)} %bitcast.546), channel_id=17, replica_groups=mesh['gx_0'=8,'gx_1'=2,'gx_2'=2,'gy_0'=2,'gy_1'=4] {'gx_0'}, dimensions={0}, use_global_device_ids=true | all-gather | bytes 9216 | tf_op jit(solution)/shard_map/all_gather | solution.py:30
  599.0 5.7 all-gather.48
  604.8 7.0 all-gather.49
  616.2 8.9 %collective-permute-done.32 = f32[3,128,256]{2,1,0:T(8,128)S(1)} collective-permute-done((f32[3,128,256]{2,1,0:T(8,128)S(1)}, f32[3,128,256]{2,1,0:T(8,128)S(1)}, u32[]{:S(2)}, u32[]{:S(2)}) %collective-permute-start.32) | collective-permute-done | bytes 393248 | tf_op jit(solution)/shard_map/ppermute | solution.py:19
  628.4 5.0 collective-permute-start.35
  639.0 5.3 collective-permute-done.36
  649.4 5.4 collective-permute-done.38
  662.5 16.7 %collective-permute-done.40 = f32[512,256]{1,0:T(8,128)S(1)} collective-permute-done((f32[512,256]{1,0:T(8,128)S(1)}, f32[512,256]{1,0:T(8,128)S(1)}, u32[]{:S(2)}, u32[]{:S(2)}) %collective-permute-start.40) | collective-permute-done | bytes 524320 | tf_op jit(solution)/shard_map/ppermute | solution.py:19
  687.7 21.2 %collective-permute-done.42 = f32[3,512,256]{2,1,0:T(8,128)S(1)} collective-permute-done((f32[3,512,256]{2,1,0:T(8,128)S(1)}, f32[3,512,256]{2,1,0:T(8,128)S(1)}, u32[]{:S(2)}, u32[]{:S(2)}) %collective-permute-start.42) | collective-permute-done | bytes 1572896 | tf_op jit(solution)/shard_map/ppermute | solution.py:25
  722.8 15.2 %all-gather.50 = f32[8,1,256]{2,1,0:T(1,128)S(1)} all-gather(f32[1,1,256]{2,1,0:T(1,128)S(1)} %bitcast.547), channel_id=22, replica_groups=mesh['gx_0'=8,'gx_1'=2,'gx_2'=2,'gy_0'=2,'gy_1'=4] {'gx_0'}, dimensions={0}, use_global_device_ids=true | all-gather | bytes 9216 | tf_op jit(solution)/shard_map/all_gather | solution.py:30
  744.8 17.0 %all-gather.53 = f32[2,1,256]{2,1,0:T(1,128)S(1)} all-gather(f32[1,1,256]{2,1,0:T(1,128)S(1)} %bitcast.430), channel_id=25, replica_groups=mesh['gx_0'=8,'gx_1'=2,'gx_2'=2,'gy_0'=2,'gy_1'=4] {'gy_0'}, dimensions={0}, use_global_device_ids=true | all-gather | bytes 3072 | tf_op jit(solution)/shard_map/all_gather | solution.py:30
  761.8 9.3 %all-gather.54 = f32[4,1,256]{2,1,0:T(1,128)S(1)} all-gather(f32[1,1,256]{2,1,0:T(1,128)S(1)} %bitcast.431), channel_id=26, replica_groups=mesh['gx_0'=8,'gx_1'=2,'gx_2'=2,'gy_0'=2,'gy_1'=4] {'gy_1'}, dimensions={0}, use_global_device_ids=true | all-gather | bytes 5120 | tf_op jit(solution)/shard_map/all_gather | solution.py:30
  771.1 13.3 %all-gather.55 = f32[8,1,256]{2,1,0:T(1,128)S(1)} all-gather(f32[1,1,256]{2,1,0:T(1,128)S(1)} %bitcast.544), channel_id=27, replica_groups=mesh['gx_0'=8,'gx_1'=2,'gx_2'=2,'gy_0'=2,'gy_1'=4] {'gx_0'}, dimensions={0}, use_global_device_ids=true | all-gather | bytes 9216 | tf_op jit(solution)/shard_map/all_gather | solution.py:30
  790.6 5.7 all-gather.58
  796.3 7.0 all-gather.59
  (346 shorter events, 249.2 us)
Async XLA Ops:
  0.7 6.9 collective-permute-start.4
  0.7 6.8 collective-permute-start.5
  3.2 16.9 %collective-permute-start = (f32[3,512]{1,0:T(4,128)S(1)}, f32[3,512]{1,0:T(4,128)S(1)}, u32[]{:S(2)}, u32[]{:S(2)}) collective-permute-start(f32[3,512]{1,0:T(4,128)S(1)} %get-tuple-element.117), channel_id=1, source_target_pairs={{0,8},{8,16},{16,24},{24,32},{32,40},{40,48},{48,56},{56,64},{64,7... | collective-permute-start | bytes 18440 | tf_op jit(solution)/shard_map/ppermute | solution.py:19
  3.4 16.6 %collective-permute-start.1 = (f32[3,512]{1,0:T(4,128)S(1)}, f32[3,512]{1,0:T(4,128)S(1)}, u32[]{:S(2)}, u32[]{:S(2)}) collective-permute-start(f32[3,512]{1,0:T(4,128)S(1)} %get-tuple-element.117), channel_id=1, source_target_pairs={{0,248},{8,0},{16,8},{24,16},{32,24},{40,32},{48,40},{56,48},{64,5... | collective-permute-start | bytes 18440 | tf_op jit(solution)/shard_map/ppermute | solution.py:19
  7.7 6.7 collective-permute-start.7
  9.0 6.3 collective-permute-start.6
  17.0 208.8 %collective-permute-start.8 = (f32[3,128,256]{2,1,0:T(8,128)}, f32[3,128,256]{2,1,0:T(8,128)}, u32[]{:S(2)}, u32[]{:S(2)}) collective-permute-start(f32[3,128,256]{2,1,0:T(8,128)} %pad_maximum_fusion.3), channel_id=1, source_target_pairs={{0,248},{8,0},{16,8},{24,16},{32,24},{40,32},{48,40},{56,48},{64,5... | collective-permute-start | bytes 1179656 | tf_op jit(solution)/shard_map/ppermute | solution.py:19
  20.1 6.6 collective-permute-start.2
  23.5 5.7 collective-permute-start.3
  25.6 200.3 %collective-permute-start.9 = (f32[3,128,256]{2,1,0:T(8,128)}, f32[3,128,256]{2,1,0:T(8,128)}, u32[]{:S(2)}, u32[]{:S(2)}) collective-permute-start(f32[3,128,256]{2,1,0:T(8,128)} %pad_maximum_fusion.4), channel_id=1, source_target_pairs={{0,8},{8,16},{16,24},{24,32},{32,40},{40,48},{48,56},{56,64},{64,7... | collective-permute-start | bytes 1179656 | tf_op jit(solution)/shard_map/ppermute | solution.py:19
  227.1 13.6 %collective-permute-start.10 = (f32[128,256]{1,0:T(8,128)S(1)}, f32[128,256]{1,0:T(8,128)S(1)}, u32[]{:S(2)}, u32[]{:S(2)}) collective-permute-start(f32[128,256]{1,0:T(8,128)S(1)} %get-tuple-element.67), channel_id=1, source_target_pairs={{1,0},{2,1},{3,2},{4,3},{5,4},{6,5},{7,6},{9,8},{10,9},{11,10},{12... | collective-permute-start | bytes 393224 | tf_op jit(solution)/shard_map/ppermute | solution.py:25
  228.4 12.3 %collective-permute-start.11 = (f32[128,256]{1,0:T(8,128)S(1)}, f32[128,256]{1,0:T(8,128)S(1)}, u32[]{:S(2)}, u32[]{:S(2)}) collective-permute-start(f32[128,256]{1,0:T(8,128)S(1)} %get-tuple-element.68), channel_id=1, source_target_pairs={{0,1},{1,2},{2,3},{3,4},{4,5},{5,6},{6,7},{8,9},{9,10},{10,11},{11... | collective-permute-start | bytes 393224 | tf_op jit(solution)/shard_map/ppermute | solution.py:25
  242.5 7.0 collective-permute-start.12
  242.6 6.9 collective-permute-start.13
  249.6 15.0 %collective-permute-start.14 = (f32[3,128,256]{2,1,0:T(8,128)S(1)}, f32[3,128,256]{2,1,0:T(8,128)S(1)}, u32[]{:S(2)}, u32[]{:S(2)}) collective-permute-start(f32[3,128,256]{2,1,0:T(8,128)S(1)} %pad_maximum_fusion.5), channel_id=1, source_target_pairs={{0,1},{1,2},{2,3},{3,4},{4,5},{5,6},{6,7},{8,9},{9,10},{10,11},{11... | collective-permute-start | bytes 1179656 | tf_op jit(solution)/shard_map/ppermute | solution.py:25
  257.3 15.3 %collective-permute-start.15 = (f32[3,128,256]{2,1,0:T(8,128)S(1)}, f32[3,128,256]{2,1,0:T(8,128)S(1)}, u32[]{:S(2)}, u32[]{:S(2)}) collective-permute-start(f32[3,128,256]{2,1,0:T(8,128)S(1)} %pad_maximum_fusion.5), channel_id=1, source_target_pairs={{1,0},{2,1},{3,2},{4,3},{5,4},{6,5},{7,6},{9,8},{10,9},{11,10},{12... | collective-permute-start | bytes 1179656 | tf_op jit(solution)/shard_map/ppermute | solution.py:25
  273.2 61.6 %copy-start.1 = (f32[512,256]{1,0:T(8,128)}, f32[512,256]{1,0:T(8,128)S(1)}, u32[]{:S(2)}) copy-start(f32[512,256]{1,0:T(8,128)S(1)} %convolution_add_fusion.5) | copy-start | bytes 1572868
  273.3 16.7 %collective-permute-start.16 = (f32[512,256]{1,0:T(8,128)S(1)}, f32[512,256]{1,0:T(8,128)S(1)}, u32[]{:S(2)}, u32[]{:S(2)}) collective-permute-start(f32[512,256]{1,0:T(8,128)S(1)} %convolution_add_fusion.5), channel_id=1, source_target_pairs={{0,8},{8,16},{16,24},{24,32},{32,40},{40,48},{48,56},{56,64},{64,7... | collective-permute-start | bytes 1572872 | tf_op jit(solution)/shard_map/ppermute | solution.py:19
  273.4 16.6 %collective-permute-start.17 = (f32[512,256]{1,0:T(8,128)S(1)}, f32[512,256]{1,0:T(8,128)S(1)}, u32[]{:S(2)}, u32[]{:S(2)}) collective-permute-start(f32[512,256]{1,0:T(8,128)S(1)} %convolution_add_fusion.5), channel_id=1, source_target_pairs={{0,248},{8,0},{16,8},{24,16},{32,24},{40,32},{48,40},{56,48},{64,5... | collective-permute-start | bytes 1572872 | tf_op jit(solution)/shard_map/ppermute | solution.py:19
  290.1 34.6 %collective-permute-start.18 = (f32[3,512,256]{2,1,0:T(8,128)S(1)}, f32[3,512,256]{2,1,0:T(8,128)S(1)}, u32[]{:S(2)}, u32[]{:S(2)}) collective-permute-start(f32[3,512,256]{2,1,0:T(8,128)S(1)} %pad_maximum_fusion), channel_id=1, source_target_pairs={{0,1},{1,2},{2,3},{3,4},{4,5},{5,6},{6,7},{8,9},{9,10},{10,11},{11... | collective-permute-start | bytes 4718600 | tf_op jit(solution)/shard_map/ppermute | solution.py:25
  295.4 35.4 %collective-permute-start.19 = (f32[3,512,256]{2,1,0:T(8,128)S(1)}, f32[3,512,256]{2,1,0:T(8,128)S(1)}, u32[]{:S(2)}, u32[]{:S(2)}) collective-permute-start(f32[3,512,256]{2,1,0:T(8,128)S(1)} %pad_maximum_fusion), channel_id=1, source_target_pairs={{1,0},{2,1},{3,2},{4,3},{5,4},{6,5},{7,6},{9,8},{10,9},{11,10},{12... | collective-permute-start | bytes 4718600 | tf_op jit(solution)/shard_map/ppermute | solution.py:25
  424.1 9.6 %collective-permute-start.20 = (f32[3,128,256]{2,1,0:T(8,128)S(1)}, f32[3,128,256]{2,1,0:T(8,128)S(1)}, u32[]{:S(2)}, u32[]{:S(2)}) collective-permute-start(f32[3,128,256]{2,1,0:T(8,128)S(1)} %pad_maximum_fusion.6), channel_id=1, source_target_pairs={{0,248},{8,0},{16,8},{24,16},{32,24},{40,32},{48,40},{56,48},{64,5... | collective-permute-start | bytes 1179656 | tf_op jit(solution)/shard_map/ppermute | solution.py:19
  424.2 10.6 %collective-permute-start.21 = (f32[3,128,256]{2,1,0:T(8,128)S(1)}, f32[3,128,256]{2,1,0:T(8,128)S(1)}, u32[]{:S(2)}, u32[]{:S(2)}) collective-permute-start(f32[3,128,256]{2,1,0:T(8,128)S(1)} %pad_maximum_fusion.7), channel_id=1, source_target_pairs={{0,8},{8,16},{16,24},{24,32},{32,40},{40,48},{48,56},{56,64},{64,7... | collective-permute-start | bytes 1179656 | tf_op jit(solution)/shard_map/ppermute | solution.py:19
  434.9 6.9 collective-permute-start.22
  436.2 7.1 collective-permute-start.23
  445.0 6.8 collective-permute-start.24
  445.1 6.7 collective-permute-start.25
  451.9 10.0 %collective-permute-start.26 = (f32[3,128,256]{2,1,0:T(8,128)S(1)}, f32[3,128,256]{2,1,0:T(8,128)S(1)}, u32[]{:S(2)}, u32[]{:S(2)}) collective-permute-start(f32[3,128,256]{2,1,0:T(8,128)S(1)} %pad_maximum_fusion.8), channel_id=1, source_target_pairs={{0,1},{1,2},{2,3},{3,4},{4,5},{5,6},{6,7},{8,9},{9,10},{10,11},{11... | collective-permute-start | bytes 1179656 | tf_op jit(solution)/shard_map/ppermute | solution.py:25
  454.9 11.1 %collective-permute-start.27 = (f32[3,128,256]{2,1,0:T(8,128)S(1)}, f32[3,128,256]{2,1,0:T(8,128)S(1)}, u32[]{:S(2)}, u32[]{:S(2)}) collective-permute-start(f32[3,128,256]{2,1,0:T(8,128)S(1)} %pad_maximum_fusion.8), channel_id=1, source_target_pairs={{1,0},{2,1},{3,2},{4,3},{5,4},{6,5},{7,6},{9,8},{10,9},{11,10},{12... | collective-permute-start | bytes 1179656 | tf_op jit(solution)/shard_map/ppermute | solution.py:25
  466.7 18.8 %collective-permute-start.28 = (f32[512,256]{1,0:T(8,128)S(1)}, f32[512,256]{1,0:T(8,128)S(1)}, u32[]{:S(2)}, u32[]{:S(2)}) collective-permute-start(f32[512,256]{1,0:T(8,128)S(1)} %convolution_add_fusion.4), channel_id=1, source_target_pairs={{0,8},{8,16},{16,24},{24,32},{32,40},{40,48},{48,56},{56,64},{64,7... | collective-permute-start | bytes 1572872 | tf_op jit(solution)/shard_map/ppermute | solution.py:19
  466.8 18.7 %collective-permute-start.29 = (f32[512,256]{1,0:T(8,128)S(1)}, f32[512,256]{1,0:T(8,128)S(1)}, u32[]{:S(2)}, u32[]{:S(2)}) collective-permute-start(f32[512,256]{1,0:T(8,128)S(1)} %convolution_add_fusion.4), channel_id=1, source_target_pairs={{0,248},{8,0},{16,8},{24,16},{32,24},{40,32},{48,40},{56,48},{64,5... | collective-permute-start | bytes 1572872 | tf_op jit(solution)/shard_map/ppermute | solution.py:19
  485.6 29.7 %collective-permute-start.30 = (f32[3,512,256]{2,1,0:T(8,128)S(1)}, f32[3,512,256]{2,1,0:T(8,128)S(1)}, u32[]{:S(2)}, u32[]{:S(2)}) collective-permute-start(f32[3,512,256]{2,1,0:T(8,128)S(1)} %pad_maximum_fusion.1), channel_id=1, source_target_pairs={{0,1},{1,2},{2,3},{3,4},{4,5},{5,6},{6,7},{8,9},{9,10},{10,11},{11... | collective-permute-start | bytes 4718600 | tf_op jit(solution)/shard_map/ppermute | solution.py:25
  487.0 35.9 %collective-permute-start.31 = (f32[3,512,256]{2,1,0:T(8,128)S(1)}, f32[3,512,256]{2,1,0:T(8,128)S(1)}, u32[]{:S(2)}, u32[]{:S(2)}) collective-permute-start(f32[3,512,256]{2,1,0:T(8,128)S(1)} %pad_maximum_fusion.1), channel_id=1, source_target_pairs={{1,0},{2,1},{3,2},{4,3},{5,4},{6,5},{7,6},{9,8},{10,9},{11,10},{12... | collective-permute-start | bytes 4718600 | tf_op jit(solution)/shard_map/ppermute | solution.py:25
  615.5 9.6 %collective-permute-start.32 = (f32[3,128,256]{2,1,0:T(8,128)S(1)}, f32[3,128,256]{2,1,0:T(8,128)S(1)}, u32[]{:S(2)}, u32[]{:S(2)}) collective-permute-start(f32[3,128,256]{2,1,0:T(8,128)S(1)} %pad_maximum_fusion.9), channel_id=1, source_target_pairs={{0,248},{8,0},{16,8},{24,16},{32,24},{40,32},{48,40},{56,48},{64,5... | collective-permute-start | bytes 1179656 | tf_op jit(solution)/shard_map/ppermute | solution.py:19
  615.7 11.3 %collective-permute-start.33 = (f32[3,128,256]{2,1,0:T(8,128)S(1)}, f32[3,128,256]{2,1,0:T(8,128)S(1)}, u32[]{:S(2)}, u32[]{:S(2)}) collective-permute-start(f32[3,128,256]{2,1,0:T(8,128)S(1)} %pad_maximum_fusion.10), channel_id=1, source_target_pairs={{0,8},{8,16},{16,24},{24,32},{32,40},{40,48},{48,56},{56,64},{64,7... | collective-permute-start | bytes 1179656 | tf_op jit(solution)/shard_map/ppermute | solution.py:19
  627.1 6.9 collective-permute-start.34
  628.4 7.1 collective-permute-start.35
  637.2 7.1 collective-permute-start.36
  637.3 7.0 collective-permute-start.37
  644.4 10.5 %collective-permute-start.38 = (f32[3,128,256]{2,1,0:T(8,128)S(1)}, f32[3,128,256]{2,1,0:T(8,128)S(1)}, u32[]{:S(2)}, u32[]{:S(2)}) collective-permute-start(f32[3,128,256]{2,1,0:T(8,128)S(1)} %pad_maximum_fusion.11), channel_id=1, source_target_pairs={{0,1},{1,2},{2,3},{3,4},{4,5},{5,6},{6,7},{8,9},{9,10},{10,11},{11... | collective-permute-start | bytes 1179656 | tf_op jit(solution)/shard_map/ppermute | solution.py:25
  647.5 12.0 %collective-permute-start.39 = (f32[3,128,256]{2,1,0:T(8,128)S(1)}, f32[3,128,256]{2,1,0:T(8,128)S(1)}, u32[]{:S(2)}, u32[]{:S(2)}) collective-permute-start(f32[3,128,256]{2,1,0:T(8,128)S(1)} %pad_maximum_fusion.11), channel_id=1, source_target_pairs={{1,0},{2,1},{3,2},{4,3},{5,4},{6,5},{7,6},{9,8},{10,9},{11,10},{12... | collective-permute-start | bytes 1179656 | tf_op jit(solution)/shard_map/ppermute | solution.py:25
  660.2 19.0 %collective-permute-start.40 = (f32[512,256]{1,0:T(8,128)S(1)}, f32[512,256]{1,0:T(8,128)S(1)}, u32[]{:S(2)}, u32[]{:S(2)}) collective-permute-start(f32[512,256]{1,0:T(8,128)S(1)} %convolution_add_fusion.3), channel_id=1, source_target_pairs={{0,8},{8,16},{16,24},{24,32},{32,40},{40,48},{48,56},{56,64},{64,7... | collective-permute-start | bytes 1572872 | tf_op jit(solution)/shard_map/ppermute | solution.py:19
  660.2 18.9 %collective-permute-start.41 = (f32[512,256]{1,0:T(8,128)S(1)}, f32[512,256]{1,0:T(8,128)S(1)}, u32[]{:S(2)}, u32[]{:S(2)}) collective-permute-start(f32[512,256]{1,0:T(8,128)S(1)} %convolution_add_fusion.3), channel_id=1, source_target_pairs={{0,248},{8,0},{16,8},{24,16},{32,24},{40,32},{48,40},{56,48},{64,5... | collective-permute-start | bytes 1572872 | tf_op jit(solution)/shard_map/ppermute | solution.py:19
  679.3 29.7 %collective-permute-start.42 = (f32[3,512,256]{2,1,0:T(8,128)S(1)}, f32[3,512,256]{2,1,0:T(8,128)S(1)}, u32[]{:S(2)}, u32[]{:S(2)}) collective-permute-start(f32[3,512,256]{2,1,0:T(8,128)S(1)} %pad_maximum_fusion.2), channel_id=1, source_target_pairs={{0,1},{1,2},{2,3},{3,4},{4,5},{5,6},{6,7},{8,9},{9,10},{10,11},{11... | collective-permute-start | bytes 4718600 | tf_op jit(solution)/shard_map/ppermute | solution.py:25
  680.7 35.3 %collective-permute-start.43 = (f32[3,512,256]{2,1,0:T(8,128)S(1)}, f32[3,512,256]{2,1,0:T(8,128)S(1)}, u32[]{:S(2)}, u32[]{:S(2)}) collective-permute-start(f32[3,512,256]{2,1,0:T(8,128)S(1)} %pad_maximum_fusion.2), channel_id=1, source_target_pairs={{1,0},{2,1},{3,2},{4,3},{5,4},{6,5},{7,6},{9,8},{10,9},{11,10},{12... | collective-permute-start | bytes 4718600 | tf_op jit(solution)/shard_map/ppermute | solution.py:25
  719.8 83.5 %copy-start.2 = (f32[512,256]{1,0:T(8,128)S(1)}, f32[512,256]{1,0:T(8,128)}, u32[]{:S(2)}) copy-start(f32[512,256]{1,0:T(8,128)} %copy-done.1) | copy-start | bytes 1572868
  719.9 83.5 %copy-start.4 = (f32[512,256]{1,0:T(8,128)S(1)}, f32[512,256]{1,0:T(8,128)}, u32[]{:S(2)}) copy-start(f32[512,256]{1,0:T(8,128)} %copy-done.3) | copy-start | bytes 1572868
  719.9 83.5 %copy-start.6 = (f32[512,256]{1,0:T(8,128)S(1)}, f32[512,256]{1,0:T(8,128)}, u32[]{:S(2)}) copy-start(f32[512,256]{1,0:T(8,128)} %get-tuple-element.135) | copy-start | bytes 1572868
  (25 other events, 365.4 us)
